TPU v7x, 32 devices: a whole 2x2x4 slice. The times are simulated.
32 devices in a mesh: lon: 4 (over y, x), lat: 8 (over z, core).
Axes of the slice: x: 2, y: 2, z: 4, core: 2. Of those that a mesh axis runs over, the one named last changes fastest.
Arguments:
- tracer: float32 [1024, 64, 128], P('lon', 'lat'), may hold values from -6 to 6
- offsets: int32 [64], P('lat'), may hold values from 0 to 1023
- frac_lon: float32 [64], P('lat'), may hold values from 0 to 1
- frac_lat: float32 [64], P('lat'), may hold values from 0 to 1
- frac_lev: float32 [64], P('lat'), may hold values from 0 to 1
- metric: float32 [64], P('lat'), may hold values from 0.5 to 2
- vertical_coef: float32 [128], replicated, may hold values from 0.5 to 4
- inverses: float32 [64, 128, 128], P('lat'), may hold values from -0.1 to 0.6, as said below
Outputs:
- advected: float32 [1024, 64, 128], P('lon', 'lat')
- pressure: float32 [1024, 64, 128], P('lon', 'lat')
- residual: float32 [1024, 64, 128], P('lon', 'lat')
Inputs may be any that keep to these rules, and one draw needn't show every extreme that they name: `inverses`: one matrix for each latitude row.
All inputs are finite; a program needn't handle non-finite values.
Results may differ from a plain program's by a relative error of at most 0.00016.
Values sent between devices are 32-bit elements; how exact they have to be, the bound alone decides.
A program may use at most 128 MiB of HBM per device.

v0:
```python
import functools

import jax
import jax.numpy as jnp
from jax import lax
from jax.experimental import pallas as pl
from jax.experimental.pallas import tpu as pltpu
from jax.sharding import PartitionSpec as P

ITERS = 3
DEEP = ITERS
PAD = 8
VM = pl.BlockSpec(memory_space=pltpu.VMEM)
SM = pl.BlockSpec(memory_space=pltpu.SMEM)
ANY = pl.BlockSpec(memory_space=pl.ANY)
F32 = jnp.float32
BF16 = jnp.bfloat16
MESH = pl.DeviceIdType.MESH


def cubic_weights(f):
    return (
        -f * (f - 1.0) * (f - 2.0) * (1.0 / 6.0),
        (f + 1.0) * (f - 1.0) * (f - 2.0) * 0.5,
        -(f + 1.0) * f * (f - 2.0) * 0.5,
        (f + 1.0) * f * (f - 1.0) * (1.0 / 6.0),
    )


def shape(*dims, dtype=F32):
    return jax.ShapeDtypeStruct(dims, dtype)


def signal(sem, peer):
    pl.semaphore_signal(sem, inc=1, device_id=peer, device_id_type=MESH)


def remote(src, dst, send_sem, recv_sem, peer):
    return pltpu.make_async_remote_copy(
        src_ref=src,
        dst_ref=dst,
        send_sem=send_sem,
        recv_sem=recv_sem,
        device_id=peer,
        device_id_type=MESH,
    )


def split(x):
    high = x.astype(BF16)
    return high, (x - high.astype(F32)).astype(BF16)


def pieces(first, last, size):
    out = []
    while first < last:
        step = size if last - first < 2 * size else size
        step = min(step, last - first)
        out.append((first, step))
        first += step
    return out


def fold(x):
    return jnp.sum(x.reshape(x.shape[0] // 8, 8, x.shape[1]), axis=0)


def coefficients(t):
    right = t[:3]
    gram = [[t[3], t[4], t[5]], [t[4], t[6], t[7]], [t[5], t[7], t[8]]]
    zero = jnp.zeros_like(t[0])

    def form(p, q):
        total = zero
        for k in range(3):
            for l in range(3):
                if p[k] is not None and q[l] is not None:
                    total = total + p[k] * q[l] * gram[k][l]
        return total

    def add(p, s, q):
        return [x if y is None else (s * y if x is None else x + s * y) for x, y in zip(p, q)]

    q = [[zero + 1.0, None, None]]
    rho, pi = [None] * 3, [None] * 3
    squares = [form(q[0], q[0])]
    for i in range(ITERS):
        along = form(q[i], rho)
        for k in range(3):
            if q[i][k] is not None:
                along = along + q[i][k] * right[k]
        alpha = along / squares[i]
        pi = add(pi, alpha, q[i])
        rho = add(rho, -alpha, q[i])
        if i + 1 < ITERS:
            z = [zero + 1.0, rho[0], rho[1]]
            new = z
            for l in range(i + 1):
                new = add(new, -form(z, q[l]) / squares[l], q[l])
            q.append(new)
            squares.append(form(new, new))
    return rho, pi


def step_kernel(lons, lats, off, f_lon, f_lat, f_lev, metric, vc_ref, tracer, inv, *refs):
    (r_ext, v0, v1, v2, w0, w1, w2, tot) = refs[:8]
    (t, double, s_buf, v_buf, g_buf, f_buf, inv_ext, met, packed, lhs, part, every) = refs[8:20]
    (t_sem, i_sem, hs, hr, ns, nr, p1s, p1r, p2s, p2r, ws, wr, es, er, fs, fr, rs, rr) = refs[20:]
    width, rows, levels = tracer.shape
    quarter = width // lons
    deep = DEEP
    ext, wide = rows + 2 * deep, width + 2 * PAD
    me, lat = lax.axis_index("lon"), lax.axis_index("lat")
    ring = lambda k: lax.rem(me + (k + lons), lons)
    has_low, has_high = lat > 0, lat < lats - 1
    below = {"lat": lax.max(lat - 1, 0)}
    above = {"lat": lax.min(lat + 1, lats - 1)}
    devices = lons * lats
    mine = me * lats + lat
    lane = lax.broadcasted_iota(jnp.int32, (1, levels), 1)

    def peer_of(k):
        index = lax.rem(mine + k, devices)
        return {"lon": lax.div(index, lats), "lat": lax.rem(index, lats)}

    first_rows = [rows - 1, 0, 1] + list(range(2, rows - 1))
    loads = {j: pltpu.make_async_copy(tracer.at[:, j, :], t.at[j + 1], t_sem.at[j]) for j in range(rows)}
    for j in first_rows:
        loads[j].start()
    matrices = pltpu.make_async_copy(inv, inv_ext.at[pl.ds(deep, rows)], i_sem)
    matrices.start()

    barrier = pltpu.get_barrier_semaphore()
    lax.fori_loop(1, devices, lambda k, c: (signal(barrier, peer_of(k)), c)[1], 0)

    for j in range(rows):
        met[deep + j : deep + j + 1, :] = jnp.full((1, levels), metric[j], F32)
        f_buf[j, :PAD, :] = jnp.zeros((PAD, levels), F32)
        f_buf[j, wide + PAD :, :] = jnp.zeros((PAD, levels), F32)
    for w in (w0, w1, w2):
        for e in range(w.shape[0]):
            w[e, :PAD, :] = jnp.zeros((PAD, levels), F32)
            w[e, wide + PAD :, :] = jnp.zeros((PAD, levels), F32)

    def clear(ref, first, count):
        ref[first : first + count] = jnp.zeros((count,) + ref.shape[1:], F32)

    @pl.when(jnp.logical_not(has_low))
    def _():
        clear(t, 0, 1)
        clear(r_ext, 0, deep)
        clear(inv_ext, 0, deep)
        met[:deep, :] = jnp.zeros((deep, levels), F32)

    @pl.when(jnp.logical_not(has_high))
    def _():
        clear(t, rows + 1, 2)
        clear(r_ext, deep + rows, deep)
        clear(inv_ext, deep + rows, deep)
        met[deep + rows : ext, :] = jnp.zeros((deep, levels), F32)

    up_row = remote(t.at[rows], t.at[0], hs.at[0], hr.at[0], above)
    down_rows = remote(t.at[pl.ds(1, 2)], t.at[pl.ds(rows + 1, 2)], hs.at[1], hr.at[1], below)
    up_inv = remote(inv_ext.at[pl.ds(rows, deep)], inv_ext.at[pl.ds(0, deep)], hs.at[2], hr.at[2], above)
    down_inv = remote(
        inv_ext.at[pl.ds(deep, deep)], inv_ext.at[pl.ds(deep + rows, deep)], hs.at[3], hr.at[3], below
    )
    up_met = [remote(met.at[rows + m], met.at[m], ns.at[m], nr.at[m], above) for m in range(deep)]
    down_met = [
        remote(met.at[deep + m], met.at[deep + rows + m], ns.at[deep + m], nr.at[deep + m], below)
        for m in range(deep)
    ]
    for j in first_rows[:3]:
        loads[j].wait()
    pl.semaphore_wait(barrier, devices - 1)

    @pl.when(has_high)
    def _():
        up_row.start()

    @pl.when(has_low)
    def _():
        down_rows.start()

    for j in first_rows[3:]:
        loads[j].wait()

    def mix(j):
        a = cubic_weights(f_lat[j])
        b = cubic_weights(f_lev[j])
        taps = {m: jnp.where((lane + m >= 0) & (lane + m < levels), b[m + 1], 0.0) for m in (-1, 1, 2)}
        buffer = double.at[j % 2]
        for first, size in pieces(0, width, 64):
            at = pl.ds(first, size)
            x = a[0] * t[j, at, :] + a[1] * t[j + 1, at, :] + a[2] * t[j + 2, at, :] + a[3] * t[j + 3, at, :]
            total = b[1] * x
            for m in (-1, 1, 2):
                total = total + taps[m] * pltpu.roll(x, (-m) % levels, 1)
            buffer[at, :] = total
            buffer[pl.ds(width + first, size), :] = total
        start = width - lax.rem(off[j], width)
        for first, size in pieces(0, width, 64):
            s_buf[j, pl.ds(first, size), :] = buffer[pl.ds(start + first, size), :]

    def part_of(device, j):
        return pl.multiple_of(lax.rem(device + j, lons) * quarter, quarter)

    def all_of(ref, j, count, send_sem, recv_sem):
        return remote(ref.at[j, pl.ds(0, count)], ref.at[j, pl.ds(0, count)], send_sem, recv_sem, {"lon": ring(1)})

    def spread(j):
        for k in range(1, lons):
            q = ring(k)
            remote(
                s_buf.at[j, pl.ds(part_of(q, j), quarter)], v_buf.at[j, me], p1s.at[j], p1r.at[j], {"lon": q}
            ).start()
        v_buf[j, me] = s_buf[j, pl.ds(part_of(me, j), quarter), :]

    def deliver(j):
        all_of(v_buf, j, lons - 1, p1s.at[j], p1r.at[j]).wait_recv()
        offset = off[j]
        rest = lax.rem(offset, width)
        block = lax.rem(lax.div(offset, width), lons)
        begin = part_of(me, j)
        some = min(32, quarter)
        for first, size in pieces(0, quarter, some):
            place = lax.broadcasted_iota(jnp.int32, (size, levels), 0) + (begin + first)
            turn = jnp.where(place < rest, lax.rem(block + 1, lons), block)
            x = [v_buf[j, s, pl.ds(first, size), :] for s in range(lons)]
            bit = lons // 2
            while bit:
                mask = (turn & bit) != 0
                x = [jnp.where(mask, x[(d - bit) % lons], x[d]) for d in range(lons)]
                bit //= 2
            for d in range(lons):
                g_buf[j, d, pl.ds(first, size), :] = x[d]
        here = pl.ds(pl.multiple_of(2 * PAD + begin, PAD), quarter)
        west = pl.ds(PAD, PAD)
        east = pl.ds(2 * PAD + width, PAD)
        for k in range(1, lons):
            d = ring(k)
            remote(g_buf.at[j, d], f_buf.at[j, here], p2s.at[j], p2r.at[j], {"lon": d}).start()
        f_buf[j, here, :] = g_buf[j, me]
        part = lax.rem(me + j, lons)

        @pl.when(part == lons - 1)
        def _():
            for k in range(1, lons):
                src = g_buf.at[j, ring(k - 1), pl.ds(quarter - PAD, PAD)]
                remote(src, f_buf.at[j, west], ws.at[j], wr.at[j], {"lon": ring(k)}).start()
            f_buf[j, west, :] = g_buf[j, ring(-1), quarter - PAD :, :]

        @pl.when(part == 0)
        def _():
            for k in range(1, lons):
                src = g_buf.at[j, ring(k + 1), pl.ds(0, PAD)]
                remote(src, f_buf.at[j, east], es.at[j], er.at[j], {"lon": ring(k)}).start()
            f_buf[j, east, :] = g_buf[j, ring(1), :PAD, :]

    def edge_wait(j, send_sem, recv_sem, owner, count):
        block = f_buf.at[j, pl.ds(PAD, PAD * count)]
        return remote(block, block, send_sem, recv_sem, {"lon": ring(1)})

    def arrive(j):
        main = f_buf.at[j, pl.ds(2 * PAD, (lons - 1) * quarter)]
        remote(main, main, p2s.at[j], p2r.at[j], {"lon": ring(1)}).wait_recv()
        part = lax.rem(me + j, lons)

        @pl.when(part != lons - 1)
        def _():
            edge_wait(j, ws.at[j], wr.at[j], lons - 1, 1).wait_recv()

        @pl.when(part != 0)
        def _():
            edge_wait(j, es.at[j], er.at[j], 0, 1).wait_recv()

        c = cubic_weights(f_lon[j])
        for first, size in pieces(0, wide, 64):
            r_ext[deep + j, pl.ds(first, size), :] = sum(
                c[m] * f_buf[j, pl.ds(first + PAD - 1 + m, size), :] for m in range(4)
            )
        if j < deep:
            @pl.when(has_low)
            def _():
                low_copy(j).start()
        if j >= rows - deep:
            @pl.when(has_high)
            def _():
                high_copy(j).start()

    def low_copy(j):
        return remote(r_ext.at[deep + j], r_ext.at[deep + rows + j], fs.at[j], fr.at[j], below)

    def high_copy(j):
        m = j - (rows - deep)
        return remote(r_ext.at[deep + j], r_ext.at[m], fs.at[deep + m], fr.at[deep + m], above)

    def settle(j):
        all_of(g_buf, j, lons - 1, p2s.at[j], p2r.at[j]).wait_send()
        all_of(v_buf, j, lons - 1, p1s.at[j], p1r.at[j]).wait_send()
        part = lax.rem(me + j, lons)

        @pl.when(part == lons - 1)
        def _():
            edge_wait(j, ws.at[j], wr.at[j], lons - 1, lons - 1).wait_send()

        @pl.when(part == 0)
        def _():
            edge_wait(j, es.at[j], er.at[j], 0, lons - 1).wait_send()

    vc = vc_ref[...]
    up = jnp.where(lane < levels - 1, vc, 0.0)
    down = jnp.where(lane > 0, vc, 0.0)
    ws_refs, vs_refs = (w0, w1, w2), (v0, v1, v2)
    acc = [jnp.zeros((8, levels), F32) for _ in range(9)]

    def pack(e):
        high, low = split(inv_ext[e])
        packed[e, :levels, :levels] = high
        packed[e, :levels, levels:] = high
        packed[e, levels:, :levels] = low
        packed[e, levels:, levels:] = jnp.zeros((levels, levels), BF16)

    def solve(k, e, slot):
        both = lax.dot_general(
            lhs[slot], packed[e], (((1,), (1,)), ((), ())), preferred_element_type=F32
        )
        ws_refs[k][e - k, pl.ds(PAD, wide), :] = both[:, :levels] + both[:, levels:]

    def load_lhs(slot, first, size, v):
        high, low = split(v)
        lhs[slot, pl.ds(first, size), :levels] = high
        lhs[slot, pl.ds(first, size), levels:] = low

    def begin(e, slot):
        for first, size in pieces(0, wide, 64):
            load_lhs(slot, first, size, r_ext[e, pl.ds(first, size), :])
        solve(0, e, slot)

    def stencil(k, e, first, size):
        w = ws_refs[k]
        n = e - k
        m = met[e : e + 1, :]
        centre = w[n, pl.ds(first + PAD, size), :]
        result = (2.0 * m + 2.1 + 2.0 * vc) * centre
        result = result - m * (
            w[n, pl.ds(first + PAD + 1, size), :] + w[n, pl.ds(first + PAD - 1, size), :]
        )
        result = result - (w[n - 1, pl.ds(first + PAD, size), :] + w[n + 1, pl.ds(first + PAD, size), :])
        result = result - up * pltpu.roll(centre, levels - 1, 1)
        return result - down * pltpu.roll(centre, 1, 1)

    pairs = {0: ((0, "r", 0), (3, 0, 0)), 1: ((1, "r", 1), (4, 0, 1), (6, 1, 1)),
             2: ((2, "r", 2), (5, 0, 2), (7, 1, 2), (8, 2, 2))}

    def apply(k, e, slot):
        inside = deep <= e < deep + rows
        if k + 1 < ITERS:
            for first, size in pieces(0, wide, 64):
                v = stencil(k, e, first, size)
                load_lhs(slot, first, size, v)
                if inside:
                    vs_refs[k][e - deep, pl.ds(first, size), :] = v
            solve(k + 1, e, slot)
            if inside:
                for first, size in pieces(PAD, PAD + width, 64):
                    gather(k, e, first, size, vs_refs[k][e - deep, pl.ds(first, size), :])
        else:
            for first, size in pieces(PAD, PAD + width, 64):
                v = stencil(k, e, first, size)
                vs_refs[k][e - deep, pl.ds(first, size), :] = v
                gather(k, e, first, size, v)

    def gather(k, e, first, size, v):
        for n, p, q in pairs[k]:
            if p == "r":
                other = r_ext[e, pl.ds(first, size), :]
            elif p == k:
                other = v
            else:
                other = vs_refs[p][e - deep, pl.ds(first, size), :]
            acc[n] = acc[n] + fold(other * v)

    plain = lambda j: 1 <= j <= rows - 3
    edges = [j for j in range(rows) if j < deep or j >= rows - deep]
    order = [j for j in edges if plain(j)] + [j for j in edges if not plain(j)]
    order += [j for j in range(rows) if j not in order]
    waited = False
    sent_inv = False
    for j in order:
        if not plain(j) and not waited:
            waited = True

            @pl.when(has_low)
            def _():
                up_row.wait_recv()

            @pl.when(has_high)
            def _():
                down_rows.wait_recv()

        mix(j)
        spread(j)
        if not sent_inv:
            sent_inv = True
            matrices.wait()

            @pl.when(has_high)
            def _():
                up_inv.start()
                for copy in up_met:
                    copy.start()

            @pl.when(has_low)
            def _():
                down_inv.start()
                for copy in down_met:
                    copy.start()

    for e in range(deep, deep + rows):
        pack(e)
    for j in order:
        deliver(j)

    @pl.when(has_low)
    def _():
        up_inv.wait_recv()
        for copy in up_met:
            copy.wait_recv()

    @pl.when(has_high)
    def _():
        down_inv.wait_recv()
        for copy in down_met:
            copy.wait_recv()

    for e in list(range(deep)) + list(range(deep + rows, ext)):
        pack(e)

    done = {}
    slots = [0]

    def slot():
        slots[0] += 1
        return slots[0] % 2

    def ready():
        again = True
        while again:
            again = False
            for k in range(ITERS):
                for e in range(k + 1, ext - k - 1):
                    if ("v", k, e) not in done and all(("w", k, e + m) in done for m in (-1, 0, 1)):
                        apply(k, e, slot())
                        done["v", k, e] = True
                        if k + 1 < ITERS:
                            done["w", k + 1, e] = True
                        again = True

    def first_solve(e):
        begin(e, slot())
        done["w", 0, e] = True

    held = order[len(edges) :]
    for j in order[: len(edges)]:
        arrive(j)
    for j in order[: len(edges)]:
        first_solve(deep + j)
    ready()
    for j in held:
        arrive(j)
        first_solve(deep + j)
    ready()

    @pl.when(has_low)
    def _():
        for m in range(deep):
            high_copy(rows - deep + m).wait_recv()

    @pl.when(has_high)
    def _():
        for m in range(deep):
            low_copy(m).wait_recv()

    for e in list(range(deep)) + list(range(deep + rows, ext)):
        first_solve(e)
    ready()

    row = jnp.zeros((1, levels), F32)
    for n in range(9):
        row = jnp.where(lane == n, jnp.sum(jnp.sum(acc[n], axis=0, keepdims=True), axis=1, keepdims=True), row)
    part[...] = row
    every[mine] = row

    def tell(k, carry):
        remote(part, every.at[mine], rs, rr, peer_of(k)).start()
        return carry

    lax.fori_loop(1, devices, tell, 0)
    for j in range(rows):
        settle(j)

    @pl.when(has_high)
    def _():
        up_row.wait_send()
        up_inv.wait_send()
        for copy in up_met:
            copy.wait_send()
        for m in range(deep):
            high_copy(rows - deep + m).wait_send()

    @pl.when(has_low)
    def _():
        down_rows.wait_send()
        down_inv.wait_send()
        for copy in down_met:
            copy.wait_send()
        for m in range(deep):
            low_copy(m).wait_send()

    others = every.at[pl.ds(0, devices - 1)]
    totals = remote(others, others, rs, rr, {"lon": ring(1)})
    totals.wait_recv()
    totals.wait_send()
    tot[...] = jnp.broadcast_to(jnp.sum(every[...], axis=0), tot.shape)


def final_kernel(tot, r_ext, v0, v1, v2, w0, w1, w2, a_out, p_out, r_out, a_buf, p_buf, r_buf, sem):
    rows = v0.shape[0]
    levels = v0.shape[2]
    width = v0.shape[1] - 2 * PAD
    deep = DEEP
    total = tot[0:1, :]
    size = min(32, width)
    copies = []

    def ship(buf, out, c, n):
        at = pl.ds(c * size * rows, size * rows)
        copy = pltpu.make_async_copy(buf.at[at], out.at[at], sem.at[n, c])
        copy.start()
        copies.append(copy)

    for c in range(width // size):
        for j in range(rows):
            a_buf[pl.ds(c * size * rows + j, size, stride=rows), :] = r_ext[
                deep + j, pl.ds(PAD + c * size, size), :
            ]
        ship(a_buf, a_out, c, 0)
    rho, pi = coefficients([total[:, n : n + 1] for n in range(9)])
    rho = [jnp.broadcast_to(x, (8, levels))[0:1] for x in rho]
    pi = [jnp.broadcast_to(x, (8, levels))[0:1] for x in pi]
    for c in range(width // size):
        for j in range(rows):
            where = pl.ds(c * size * rows + j, size, stride=rows)
            at = pl.ds(PAD + c * size, size)
            wat = pl.ds(2 * PAD + c * size, size)
            p_buf[where, :] = (
                pi[0] * w0[deep + j, wat, :] + pi[1] * w1[deep - 1 + j, wat, :] + pi[2] * w2[deep - 2 + j, wat, :]
            )
            r_buf[where, :] = r_ext[deep + j, at, :] + (
                rho[0] * v0[j, at, :] + rho[1] * v1[j, at, :] + rho[2] * v2[j, at, :]
            )
        ship(p_buf, p_out, c, 1)
        ship(r_buf, r_out, c, 2)
    for copy in copies:
        copy.wait()


def body(tracer, offsets, frac_lon, frac_lat, frac_lev, metric, vertical_coef, inverses):
    width, rows, levels = tracer.shape
    lons, lats = lax.axis_size("lon"), lax.axis_size("lat")
    deep = DEEP
    ext, wide, quarter = rows + 2 * deep, width + 2 * PAD, width // lons
    devices = lons * lats
    dma = pltpu.SemaphoreType.DMA
    field = [shape(rows, wide, levels)] * 3
    sides = [shape(ext - 2 * k, wide + 2 * PAD, levels) for k in range(3)]
    r_ext, v0, v1, v2, w0, w1, w2, tot = pl.pallas_call(
        functools.partial(step_kernel, lons, lats),
        out_shape=[shape(ext, wide, levels)] + field + sides + [shape(8, levels)],
        in_specs=[SM] * 5 + [VM, ANY, ANY],
        out_specs=[VM] * 8,
        scratch_shapes=[
            pltpu.VMEM((rows + 3, width, levels), F32),
            pltpu.VMEM((2, 2 * width, levels), F32),
            pltpu.VMEM((rows, width, levels), F32),
            pltpu.VMEM((rows, lons, quarter, levels), F32),
            pltpu.VMEM((rows, lons, quarter, levels), F32),
            pltpu.VMEM((rows, wide + 2 * PAD, levels), F32),
            pltpu.VMEM((ext, levels, levels), F32),
            pltpu.VMEM((ext, levels), F32),
            pltpu.VMEM((ext, 2 * levels, 2 * levels), BF16),
            pltpu.VMEM((2, wide, 2 * levels), BF16),
            pltpu.VMEM((1, levels), F32),
            pltpu.VMEM((devices, 1, levels), F32),
            dma((rows,)),
            dma,
            dma((4,)),
            dma((4,)),
            dma((2 * deep,)),
            dma((2 * deep,)),
        ]
        + [dma((rows,))] * 8
        + [dma((2 * deep,))] * 2
        + [dma] * 2,
        compiler_params=pltpu.CompilerParams(
            collective_id=1, has_side_effects=True, vmem_limit_bytes=30 * 2**20
        ),
    )(offsets, frac_lon, frac_lat, frac_lev, metric, vertical_coef.reshape(1, levels), tracer, inverses)
    whole = shape(width * rows, levels)
    buffer = pltpu.VMEM((width * rows, levels), F32)
    outs = pl.pallas_call(
        final_kernel,
        out_shape=[whole] * 3,
        in_specs=[VM] * 8,
        out_specs=[ANY] * 3,
        scratch_shapes=[buffer] * 3 + [dma((3, width // min(32, width)))],
        compiler_params=pltpu.CompilerParams(vmem_limit_bytes=20 * 2**20),
    )(tot, r_ext, v0, v1, v2, w0, w1, w2)
    return tuple(x.reshape(width, rows, levels) for x in outs)


def solution(mesh):
    cube = P("lon", "lat", None)
    in_specs = (cube, P("lat"), P("lat"), P("lat"), P("lat"), P("lat"), P(), P("lat", None, None))
    return jax.shard_map(
        body, mesh=mesh, in_specs=in_specs, out_specs=(cube, cube, cube), check_vma=False
    )
```

profile of v0, /device:TPU:0, one launch (start us, length us, event | category | flops | bytes accessed | tf_op | source)
XLA Modules:
  0.0 51.9 jit_solution(3944641140371868316)
XLA Ops:
  0.6 0.0 copy-start
  0.6 1.2 %copy-done = f32[256,8,128]{2,1,0:T(8,128)S(1)} copy-done((f32[256,8,128]{2,1,0:T(8,128)S(1)}, f32[256,8,128]{2,1,0:T(8,128)}, u32[]{:S(2)}) %copy-start) | copy-done | bytes 1048600
  1.9 0.0 copy-start.1
  1.9 1.0 %copy-done.1 = f32[8,128,128]{2,1,0:T(8,128)S(1)} copy-done((f32[8,128,128]{2,1,0:T(8,128)S(1)}, f32[8,128,128]{2,1,0:T(8,128)}, u32[]{:S(2)}) %copy-start.1) | copy-done | bytes 524312
  2.9 0.0 copy-start.2
  2.9 0.7 %copy-done.2 = s32[8]{0:T(128)S(1)} copy-done((s32[8]{0:T(128)S(1)}, s32[8]{0:T(128)}, u32[]{:S(2)}) %copy-start.2) | copy-done | bytes 56
  3.6 0.0 copy-start.3
  3.6 0.7 %copy-done.3 = f32[8]{0:T(128)S(1)} copy-done((f32[8]{0:T(128)S(1)}, f32[8]{0:T(128)}, u32[]{:S(2)}) %copy-start.3) | copy-done | bytes 56
  4.2 0.0 copy-start.4
  4.2 0.7 %copy-done.4 = f32[8]{0:T(128)S(1)} copy-done((f32[8]{0:T(128)S(1)}, f32[8]{0:T(128)}, u32[]{:S(2)}) %copy-start.4) | copy-done | bytes 56
  4.9 0.0 copy-start.5
  4.9 0.7 %copy-done.5 = f32[8]{0:T(128)S(1)} copy-done((f32[8]{0:T(128)S(1)}, f32[8]{0:T(128)}, u32[]{:S(2)}) %copy-start.5) | copy-done | bytes 56
  5.5 0.0 copy-start.6
  5.5 0.7 %copy-done.6 = f32[8]{0:T(128)S(1)} copy-done((f32[8]{0:T(128)S(1)}, f32[8]{0:T(128)}, u32[]{:S(2)}) %copy-start.6) | copy-done | bytes 56
  6.2 0.0 copy-start.7
  6.2 0.7 %copy-done.7 = f32[128]{0:T(128)S(1)} copy-done((f32[128]{0:T(128)S(1)}, f32[128]{0:T(128)}, u32[]{:S(2)}) %copy-start.7) | copy-done | bytes 536
  6.8 42.8 %shard_map.103 = (f32[14,272,128]{2,1,0:T(8,128)S(1)}, f32[8,272,128]{2,1,0:T(8,128)S(1)}, f32[8,272,128]{2,1,0:T(8,128)S(1)}, f32[8,272,128]{2,1,0:T(8,128)S(1)...) custom-call(s32[8]{0:T(128)S(1)} %copy-done.2, ...), custom_call_target="tpu_custom_call" | custom-call | tf_op jit(solution)/shard_map/pallas_call | solution.py:578
  49.6 2.3 %shard_map.104 = (f32[2048,128]{1,0:T(8,128)}, f32[2048,128]{1,0:T(8,128)}, f32[2048,128]{1,0:T(8,128)}) custom-call(f32[8,128]{1,0:T(8,128)S(1)} %get-tuple-element.14.tot, f32[14,272,128]{2,1,0:T(8,128)S(1)} %get-tuple-element.15.r_ext, f32[8,272,128]{2,1,0:T(8,128)S(1)} %get-tuple-element.16.v0, f32[8,272,128]{2,1,0:T(8,128)S(1)} %get-tuple-element.17.v1, ...), custom_call_target="tpu_custom_call" | custom-call | tf_op jit(solution)/shard_map/pallas_call | solution.py:612
Async XLA Ops:
  0.6 1.2 %copy-start = (f32[256,8,128]{2,1,0:T(8,128)S(1)}, f32[256,8,128]{2,1,0:T(8,128)}, u32[]{:S(2)}) copy-start(f32[256,8,128]{2,1,0:T(8,128)} %tracer.1) | copy-start | bytes 3145732
  1.9 1.0 %copy-start.1 = (f32[8,128,128]{2,1,0:T(8,128)S(1)}, f32[8,128,128]{2,1,0:T(8,128)}, u32[]{:S(2)}) copy-start(f32[8,128,128]{2,1,0:T(8,128)} %inv.1) | copy-start | bytes 1572868
  2.9 0.7 %copy-start.2 = (s32[8]{0:T(128)S(1)}, s32[8]{0:T(128)}, u32[]{:S(2)}) copy-start(s32[8]{0:T(128)} %off.1) | copy-start | bytes 100
  3.6 0.7 %copy-start.3 = (f32[8]{0:T(128)S(1)}, f32[8]{0:T(128)}, u32[]{:S(2)}) copy-start(f32[8]{0:T(128)} %f_lon.1) | copy-start | bytes 100
  4.2 0.7 %copy-start.4 = (f32[8]{0:T(128)S(1)}, f32[8]{0:T(128)}, u32[]{:S(2)}) copy-start(f32[8]{0:T(128)} %f_lat.1) | copy-start | bytes 100
  4.9 0.7 %copy-start.5 = (f32[8]{0:T(128)S(1)}, f32[8]{0:T(128)}, u32[]{:S(2)}) copy-start(f32[8]{0:T(128)} %f_lev.1) | copy-start | bytes 100
  5.5 0.7 %copy-start.6 = (f32[8]{0:T(128)S(1)}, f32[8]{0:T(128)}, u32[]{:S(2)}) copy-start(f32[8]{0:T(128)} %metric.1) | copy-start | bytes 100
  6.2 0.7 %copy-start.7 = (f32[128]{0:T(128)S(1)}, f32[128]{0:T(128)}, u32[]{:S(2)}) copy-start(f32[128]{0:T(128)} %param.14) | copy-start | bytes 1540
where the time goes:
time: 52.2 us; the launch traced here: 51.9 us
  Pallas kernels  45.1 us (86%)
  local copies, waits for them, and re-layouts  6.19 us (12%)
  between operations  0.66 us (1%)
    pallas_call x1, Pallas kernels, body(): pl.pallas_call(functools.partial(step_kernel, lons, lats), out_shape=[sha...  42.8 us
    unnamed x16, local copies, waits for them, and re-layouts  6.19 us
    pallas_call x1, Pallas kernels, body(): pl.pallas_call(final_kernel, out_shape=[whole] * 3, in_specs=[VM] * 8, ou...  2.32 us

commit v1 on v0

--- a/solution.py
+++ b/solution.py
@@ -11,8 +11,8 @@
 DEEP = ITERS
 PAD = 8
 VM = pl.BlockSpec(memory_space=pltpu.VMEM)
-SM = pl.BlockSpec(memory_space=pltpu.SMEM)
 ANY = pl.BlockSpec(memory_space=pl.ANY)
+HBM = pl.BlockSpec(memory_space=pltpu.HBM)
 F32 = jnp.float32
 BF16 = jnp.bfloat16
 MESH = pl.DeviceIdType.MESH
@@ -102,9 +102,11 @@
     return rho, pi
 
 
-def step_kernel(lons, lats, off, f_lon, f_lat, f_lev, metric, vc_ref, tracer, inv, *refs):
+def step_kernel(lons, lats, *refs):
+    scalars, (tracer, inv), refs = refs[:6], refs[6:8], refs[8:]
     (r_ext, v0, v1, v2, w0, w1, w2, tot) = refs[:8]
     (t, double, s_buf, v_buf, g_buf, f_buf, inv_ext, met, packed, lhs, part, every) = refs[8:20]
+    (off, f_lon, f_lat, f_lev, metric, vc_ref, c_sem), refs = refs[20:27], refs[:20] + refs[27:]
     (t_sem, i_sem, hs, hr, ns, nr, p1s, p1r, p2s, p2r, ws, wr, es, er, fs, fr, rs, rr) = refs[20:]
     width, rows, levels = tracer.shape
     quarter = width // lons
@@ -127,12 +129,20 @@
     loads = {j: pltpu.make_async_copy(tracer.at[:, j, :], t.at[j + 1], t_sem.at[j]) for j in range(rows)}
     for j in first_rows:
         loads[j].start()
+    fetches = [
+        pltpu.make_async_copy(src, dst, c_sem.at[n])
+        for n, (src, dst) in enumerate(zip(scalars, (off, f_lon, f_lat, f_lev, metric, vc_ref)))
+    ]
+    for copy in fetches:
+        copy.start()
     matrices = pltpu.make_async_copy(inv, inv_ext.at[pl.ds(deep, rows)], i_sem)
     matrices.start()
 
     barrier = pltpu.get_barrier_semaphore()
     lax.fori_loop(1, devices, lambda k, c: (signal(barrier, peer_of(k)), c)[1], 0)
 
+    for copy in fetches:
+        copy.wait()
     for j in range(rows):
         met[deep + j : deep + j + 1, :] = jnp.full((1, levels), metric[j], F32)
         f_buf[j, :PAD, :] = jnp.zeros((PAD, levels), F32)
@@ -575,10 +585,12 @@
     dma = pltpu.SemaphoreType.DMA
     field = [shape(rows, wide, levels)] * 3
     sides = [shape(ext - 2 * k, wide + 2 * PAD, levels) for k in range(3)]
+    arguments = (offsets, frac_lon, frac_lat, frac_lev, metric, vertical_coef.reshape(1, levels), tracer, inverses)
+    arguments = [pltpu.with_memory_space_constraint(x, pltpu.HBM) for x in arguments]
     r_ext, v0, v1, v2, w0, w1, w2, tot = pl.pallas_call(
         functools.partial(step_kernel, lons, lats),
         out_shape=[shape(ext, wide, levels)] + field + sides + [shape(8, levels)],
-        in_specs=[SM] * 5 + [VM, ANY, ANY],
+        in_specs=[HBM] * 8,
         out_specs=[VM] * 8,
         scratch_shapes=[
             pltpu.VMEM((rows + 3, width, levels), F32),
@@ -593,6 +605,12 @@
             pltpu.VMEM((2, wide, 2 * levels), BF16),
             pltpu.VMEM((1, levels), F32),
             pltpu.VMEM((devices, 1, levels), F32),
+            pltpu.SMEM((rows,), jnp.int32),
+        ]
+        + [pltpu.SMEM((rows,), F32)] * 4
+        + [
+            pltpu.VMEM((1, levels), F32),
+            dma((6,)),
             dma((rows,)),
             dma,
             dma((4,)),
@@ -606,7 +624,7 @@
         compiler_params=pltpu.CompilerParams(
             collective_id=1, has_side_effects=True, vmem_limit_bytes=30 * 2**20
         ),
-    )(offsets, frac_lon, frac_lat, frac_lev, metric, vertical_coef.reshape(1, levels), tracer, inverses)
+    )(*arguments)
     whole = shape(width * rows, levels)
     buffer = pltpu.VMEM((width * rows, levels), F32)
     outs = pl.pallas_call(

time: 52.2 us -> 44 us (0.84)
  local copies, waits for them, and re-layouts: 6.19 us -> 0 us
  Pallas kernels: 45.1 us -> 43.2 us
    unnamed x16 -> x0, local copies, waits for them, and re-layouts: 6.19 us -> none
    pallas_call x1, Pallas kernels: 42.8 us -> 40.9 us  [body(): pl.pallas_call(functools.partial(step_kernel, lons, lats), out_shape=[sha...]
where the time goes in v1:
time: 44 us; the launch traced here: 43.9 us
  Pallas kernels  43.2 us (98%)
  between operations  0.64 us (1%)
    pallas_call x1, Pallas kernels, body(): pl.pallas_call(functools.partial(step_kernel, lons, lats), out_shape=[sha...  40.9 us
    pallas_call x1, Pallas kernels, body(): pl.pallas_call(final_kernel, out_shape=[whole] * 3, in_specs=[VM] * 8, ou...  2.32 us

profile of v1, /device:TPU:0, one launch (start us, length us, event | category | flops | bytes accessed | tf_op | source)
XLA Modules:
  0.0 43.9 jit_solution(11694585338693015090)
XLA Ops:
  0.6 40.9 %shard_map.103 = (f32[14,272,128]{2,1,0:T(8,128)S(1)}, f32[8,272,128]{2,1,0:T(8,128)S(1)}, f32[8,272,128]{2,1,0:T(8,128)S(1)}, f32[8,272,128]{2,1,0:T(8,128)S(1)...) custom-call(s32[8]{0:T(128)} %refs_0_.1, ...), custom_call_target="tpu_custom_call" | custom-call | tf_op jit(solution)/shard_map/pallas_call | solution.py:590
  41.6 2.3 %shard_map.104 = (f32[2048,128]{1,0:T(8,128)}, f32[2048,128]{1,0:T(8,128)}, f32[2048,128]{1,0:T(8,128)}) custom-call(f32[8,128]{1,0:T(8,128)S(1)} %get-tuple-element.14.tot, f32[14,272,128]{2,1,0:T(8,128)S(1)} %get-tuple-element.15.r_ext, f32[8,272,128]{2,1,0:T(8,128)S(1)} %get-tuple-element.16.v0, f32[8,272,128]{2,1,0:T(8,128)S(1)} %get-tuple-element.17.v1, ...), custom_call_target="tpu_custom_call" | custom-call | tf_op jit(solution)/shard_map/pallas_call | solution.py:630

commit v2 on v1

--- a/solution.py
+++ b/solution.py
@@ -104,10 +104,12 @@
 
 def step_kernel(lons, lats, *refs):
     scalars, (tracer, inv), refs = refs[:6], refs[6:8], refs[8:]
-    (r_ext, v0, v1, v2, w0, w1, w2, tot) = refs[:8]
-    (t, double, s_buf, v_buf, g_buf, f_buf, inv_ext, met, packed, lhs, part, every) = refs[8:20]
-    (off, f_lon, f_lat, f_lev, metric, vc_ref, c_sem), refs = refs[20:27], refs[:20] + refs[27:]
-    (t_sem, i_sem, hs, hr, ns, nr, p1s, p1r, p2s, p2r, ws, wr, es, er, fs, fr, rs, rr) = refs[20:]
+    flat, tot, refs = refs[:7], refs[7], refs[8:]
+    (r_ext, v0, v1, v2, w0, w1, w2, z0, z1, z2), refs = refs[:10], refs[10:]
+    (t, double, s_buf, v_buf, g_buf, f_buf, inv_ext, met), refs = refs[:8], refs[8:]
+    (column, packed, extra, lhs, part, every), refs = refs[:6], refs[6:]
+    (off, f_lon, f_lat, f_lev, metric, vc_ref, c_sem), refs = refs[:7], refs[7:]
+    (t_sem, i_sem, hs, hr, ns, nr, p1s, p1r, p2s, p2r, ws, wr, es, er, fs, fr, rs, rr) = refs
     width, rows, levels = tracer.shape
     quarter = width // lons
     deep = DEEP
@@ -145,12 +147,15 @@
         copy.wait()
     for j in range(rows):
         met[deep + j : deep + j + 1, :] = jnp.full((1, levels), metric[j], F32)
-        f_buf[j, :PAD, :] = jnp.zeros((PAD, levels), F32)
-        f_buf[j, wide + PAD :, :] = jnp.zeros((PAD, levels), F32)
-    for w in (w0, w1, w2):
-        for e in range(w.shape[0]):
-            w[e, :PAD, :] = jnp.zeros((PAD, levels), F32)
-            w[e, wide + PAD :, :] = jnp.zeros((PAD, levels), F32)
+
+    def clear_pads():
+        for j in range(rows):
+            f_buf[j, :PAD, :] = jnp.zeros((PAD, levels), F32)
+            f_buf[j, wide + PAD :, :] = jnp.zeros((PAD, levels), F32)
+        for w in (w0, w1, w2):
+            for e in range(w.shape[0]):
+                w[e, :PAD, :] = jnp.zeros((PAD, levels), F32)
+                w[e, wide + PAD :, :] = jnp.zeros((PAD, levels), F32)
 
     def clear(ref, first, count):
         ref[first : first + count] = jnp.zeros((count,) + ref.shape[1:], F32)
@@ -318,24 +323,35 @@
         def _():
             edge_wait(j, es.at[j], er.at[j], 0, lons - 1).wait_send()
 
-    vc = vc_ref[...]
-    up = jnp.where(lane < levels - 1, vc, 0.0)
-    down = jnp.where(lane > 0, vc, 0.0)
-    ws_refs, vs_refs = (w0, w1, w2), (v0, v1, v2)
+    ws_refs, vs_refs, zs_refs = (w0, w1, w2), (v0, v1, v2), (z0, z1, z2)
     acc = [jnp.zeros((8, levels), F32) for _ in range(9)]
+    lines = 32
+
+    def turn_coefficients():
+        tall = jnp.broadcast_to(vc_ref[...], (levels, levels)).T
+        place = lax.broadcasted_iota(jnp.int32, (levels, levels), 0)
+        column[0] = 2.1 + 2.0 * tall
+        column[1] = jnp.where(place < levels - 1, tall, 0.0)
+        column[2] = jnp.where(place > 0, tall, 0.0)
 
     def pack(e):
-        high, low = split(inv_ext[e])
-        packed[e, :levels, :levels] = high
-        packed[e, :levels, levels:] = high
-        packed[e, levels:, :levels] = low
-        packed[e, levels:, levels:] = jnp.zeros((levels, levels), BF16)
+        matrix = inv_ext[e]
+        applied = column[0] * matrix - column[1] * pltpu.roll(matrix, levels - 1, 0)
+        applied = applied - column[2] * pltpu.roll(matrix, 1, 0)
+        for n, x in enumerate((matrix, applied)):
+            high, low = split(x)
+            at = pl.ds(n * levels, levels)
+            packed[e, at, :levels] = high
+            packed[e, at, levels:] = high
+            extra[e, at, :] = low
 
     def solve(k, e, slot):
-        both = lax.dot_general(
-            lhs[slot], packed[e], (((1,), (1,)), ((), ())), preferred_element_type=F32
-        )
-        ws_refs[k][e - k, pl.ds(PAD, wide), :] = both[:, :levels] + both[:, levels:]
+        dims = (((1,), (1,)), ((), ()))
+        both = lax.dot_general(lhs[slot], packed[e], dims, preferred_element_type=F32)
+        both = both + lax.dot_general(lhs[slot, :, :levels], extra[e], dims, preferred_element_type=F32)
+        ws_refs[k][e - k, pl.ds(PAD, wide), :] = both[:, :levels]
+        if k < e < ext - k - 1:
+            zs_refs[k][e - k - 1] = both[:, levels:]
 
     def load_lhs(slot, first, size, v):
         high, low = split(v)
@@ -343,7 +359,7 @@
         lhs[slot, pl.ds(first, size), levels:] = low
 
     def begin(e, slot):
-        for first, size in pieces(0, wide, 64):
+        for first, size in pieces(0, wide, lines):
             load_lhs(slot, first, size, r_ext[e, pl.ds(first, size), :])
         solve(0, e, slot)
 
@@ -351,14 +367,12 @@
         w = ws_refs[k]
         n = e - k
         m = met[e : e + 1, :]
-        centre = w[n, pl.ds(first + PAD, size), :]
-        result = (2.0 * m + 2.1 + 2.0 * vc) * centre
+        at = pl.ds(first + PAD, size)
+        result = zs_refs[k][n - 1, pl.ds(first, size), :] + (2.0 * m) * w[n, at, :]
         result = result - m * (
             w[n, pl.ds(first + PAD + 1, size), :] + w[n, pl.ds(first + PAD - 1, size), :]
         )
-        result = result - (w[n - 1, pl.ds(first + PAD, size), :] + w[n + 1, pl.ds(first + PAD, size), :])
-        result = result - up * pltpu.roll(centre, levels - 1, 1)
-        return result - down * pltpu.roll(centre, 1, 1)
+        return result - (w[n - 1, at, :] + w[n + 1, at, :])
 
     pairs = {0: ((0, "r", 0), (3, 0, 0)), 1: ((1, "r", 1), (4, 0, 1), (6, 1, 1)),
              2: ((2, "r", 2), (5, 0, 2), (7, 1, 2), (8, 2, 2))}
@@ -366,17 +380,17 @@
     def apply(k, e, slot):
         inside = deep <= e < deep + rows
         if k + 1 < ITERS:
-            for first, size in pieces(0, wide, 64):
+            for first, size in pieces(0, wide, lines):
                 v = stencil(k, e, first, size)
                 load_lhs(slot, first, size, v)
                 if inside:
                     vs_refs[k][e - deep, pl.ds(first, size), :] = v
             solve(k + 1, e, slot)
             if inside:
-                for first, size in pieces(PAD, PAD + width, 64):
+                for first, size in pieces(PAD, PAD + width, lines):
                     gather(k, e, first, size, vs_refs[k][e - deep, pl.ds(first, size), :])
         else:
-            for first, size in pieces(PAD, PAD + width, 64):
+            for first, size in pieces(PAD, PAD + width, lines):
                 v = stencil(k, e, first, size)
                 vs_refs[k][e - deep, pl.ds(first, size), :] = v
                 gather(k, e, first, size, v)
@@ -395,6 +409,8 @@
     edges = [j for j in range(rows) if j < deep or j >= rows - deep]
     order = [j for j in edges if plain(j)] + [j for j in edges if not plain(j)]
     order += [j for j in range(rows) if j not in order]
+    outer = sorted(edges, key=lambda j: min(j, rows - 1 - j))
+    later = outer + [j for j in range(rows) if j not in outer]
     waited = False
     sent_inv = False
     for j in order:
@@ -427,10 +443,12 @@
                 for copy in down_met:
                     copy.start()
 
+    clear_pads()
+    turn_coefficients()
+    for j in later:
+        deliver(j)
     for e in range(deep, deep + rows):
         pack(e)
-    for j in order:
-        deliver(j)
 
     @pl.when(has_low)
     def _():
@@ -471,29 +489,29 @@
         begin(e, slot())
         done["w", 0, e] = True
 
-    held = order[len(edges) :]
-    for j in order[: len(edges)]:
-        arrive(j)
-    for j in order[: len(edges)]:
-        first_solve(deep + j)
-    ready()
-    for j in held:
+    def halo_rows(m):
+        @pl.when(has_low)
+        def _():
+            high_copy(rows - 1 - m).wait_recv()
+
+        @pl.when(has_high)
+        def _():
+            low_copy(m).wait_recv()
+
+        for e in (deep - 1 - m, deep + rows + m):
+            first_solve(e)
+
+    for n, j in enumerate(outer):
         arrive(j)
         first_solve(deep + j)
-    ready()
-
-    @pl.when(has_low)
-    def _():
-        for m in range(deep):
-            high_copy(rows - deep + m).wait_recv()
-
-    @pl.when(has_high)
-    def _():
-        for m in range(deep):
-            low_copy(m).wait_recv()
-
-    for e in list(range(deep)) + list(range(deep + rows, ext)):
-        first_solve(e)
+        if n % 2 == 1 and n >= 3:
+            halo_rows(n // 2 - 1)
+        ready()
+    for j in later[len(outer) :]:
+        arrive(j)
+        first_solve(deep + j)
+        ready()
+    halo_rows(deep - 1)
     ready()
 
     row = jnp.zeros((1, levels), F32)
@@ -502,11 +520,28 @@
     part[...] = row
     every[mine] = row
 
-    def tell(k, carry):
+    def tell(a, b):
+        to = {"lon": ring(a), "lat": lax.rem(lat + b, lats)}
+        remote(part, every.at[mine], rs, rr, to).start()
+
+    def tell_rest(k, carry):
         remote(part, every.at[mine], rs, rr, peer_of(k)).start()
         return carry
 
-    lax.fori_loop(1, devices, tell, 0)
+    if devices <= 64:
+        far = lambda n, count: sorted(range(n), key=lambda k: abs(k - n // 2))
+        for b in far(lats, lats):
+            for a in far(lons, lons):
+                if a or b:
+                    tell(a, b)
+    else:
+        lax.fori_loop(1, devices, tell_rest, 0)
+    for j in range(rows):
+        where = pl.ds(j, width, stride=rows)
+        flat[0][where, :] = r_ext[deep + j, pl.ds(PAD, width), :]
+        for k in range(ITERS):
+            flat[1 + k][where, :] = vs_refs[k][j, pl.ds(PAD, width), :]
+            flat[4 + k][where, :] = ws_refs[k][deep + j - k, pl.ds(2 * PAD, width), :]
     for j in range(rows):
         settle(j)
 
@@ -535,45 +570,23 @@
     tot[...] = jnp.broadcast_to(jnp.sum(every[...], axis=0), tot.shape)
 
 
-def final_kernel(tot, r_ext, v0, v1, v2, w0, w1, w2, a_out, p_out, r_out, a_buf, p_buf, r_buf, sem):
-    rows = v0.shape[0]
-    levels = v0.shape[2]
-    width = v0.shape[1] - 2 * PAD
-    deep = DEEP
+def final_kernel(size, tot, r, v0, v1, v2, w0, w1, w2, a_out, p_out, r_out, p_buf, r_buf, a_sem, sem):
+    advected = pltpu.make_async_copy(r, a_out, a_sem)
+    advected.start()
     total = tot[0:1, :]
-    size = min(32, width)
+    rho, pi = coefficients([jnp.broadcast_to(total[:, n : n + 1], total.shape) for n in range(9)])
     copies = []
-
-    def ship(buf, out, c, n):
-        at = pl.ds(c * size * rows, size * rows)
-        copy = pltpu.make_async_copy(buf.at[at], out.at[at], sem.at[n, c])
-        copy.start()
-        copies.append(copy)
-
-    for c in range(width // size):
-        for j in range(rows):
-            a_buf[pl.ds(c * size * rows + j, size, stride=rows), :] = r_ext[
-                deep + j, pl.ds(PAD + c * size, size), :
-            ]
-        ship(a_buf, a_out, c, 0)
-    rho, pi = coefficients([total[:, n : n + 1] for n in range(9)])
-    rho = [jnp.broadcast_to(x, (8, levels))[0:1] for x in rho]
-    pi = [jnp.broadcast_to(x, (8, levels))[0:1] for x in pi]
-    for c in range(width // size):
-        for j in range(rows):
-            where = pl.ds(c * size * rows + j, size, stride=rows)
-            at = pl.ds(PAD + c * size, size)
-            wat = pl.ds(2 * PAD + c * size, size)
-            p_buf[where, :] = (
-                pi[0] * w0[deep + j, wat, :] + pi[1] * w1[deep - 1 + j, wat, :] + pi[2] * w2[deep - 2 + j, wat, :]
-            )
-            r_buf[where, :] = r_ext[deep + j, at, :] + (
-                rho[0] * v0[j, at, :] + rho[1] * v1[j, at, :] + rho[2] * v2[j, at, :]
-            )
-        ship(p_buf, p_out, c, 1)
-        ship(r_buf, r_out, c, 2)
+    for c in range(r.shape[0] // size):
+        at = pl.ds(c * size, size)
+        p_buf[at, :] = pi[0] * w0[at, :] + pi[1] * w1[at, :] + pi[2] * w2[at, :]
+        r_buf[at, :] = r[at, :] + (rho[0] * v0[at, :] + rho[1] * v1[at, :] + rho[2] * v2[at, :])
+        for n, (src, dst) in enumerate(((p_buf, p_out), (r_buf, r_out))):
+            copy = pltpu.make_async_copy(src.at[at], dst.at[at], sem.at[n, c])
+            copy.start()
+            copies.append(copy)
     for copy in copies:
         copy.wait()
+    advected.wait()
 
 
 def body(tracer, offsets, frac_lon, frac_lat, frac_lev, metric, vertical_coef, inverses):
@@ -583,16 +596,22 @@
     ext, wide, quarter = rows + 2 * deep, width + 2 * PAD, width // lons
     devices = lons * lats
     dma = pltpu.SemaphoreType.DMA
-    field = [shape(rows, wide, levels)] * 3
-    sides = [shape(ext - 2 * k, wide + 2 * PAD, levels) for k in range(3)]
+    whole = shape(width * rows, levels)
+    field = [pltpu.VMEM((rows, wide, levels), F32)] * 3
+    sides = [pltpu.VMEM((ext - 2 * k, wide + 2 * PAD, levels), F32) for k in range(3)]
+    verticals = [pltpu.VMEM((ext - 2 * k - 2, wide, levels), F32) for k in range(3)]
     arguments = (offsets, frac_lon, frac_lat, frac_lev, metric, vertical_coef.reshape(1, levels), tracer, inverses)
     arguments = [pltpu.with_memory_space_constraint(x, pltpu.HBM) for x in arguments]
-    r_ext, v0, v1, v2, w0, w1, w2, tot = pl.pallas_call(
+    *flat, tot = pl.pallas_call(
         functools.partial(step_kernel, lons, lats),
-        out_shape=[shape(ext, wide, levels)] + field + sides + [shape(8, levels)],
+        out_shape=[whole] * 7 + [shape(8, levels)],
         in_specs=[HBM] * 8,
         out_specs=[VM] * 8,
-        scratch_shapes=[
+        scratch_shapes=[pltpu.VMEM((ext, wide, levels), F32)]
+        + field
+        + sides
+        + verticals
+        + [
             pltpu.VMEM((rows + 3, width, levels), F32),
             pltpu.VMEM((2, 2 * width, levels), F32),
             pltpu.VMEM((rows, width, levels), F32),
@@ -601,7 +620,9 @@
             pltpu.VMEM((rows, wide + 2 * PAD, levels), F32),
             pltpu.VMEM((ext, levels, levels), F32),
             pltpu.VMEM((ext, levels), F32),
+            pltpu.VMEM((3, levels, levels), F32),
             pltpu.VMEM((ext, 2 * levels, 2 * levels), BF16),
+            pltpu.VMEM((ext, 2 * levels, levels), BF16),
             pltpu.VMEM((2, wide, 2 * levels), BF16),
             pltpu.VMEM((1, levels), F32),
             pltpu.VMEM((devices, 1, levels), F32),
@@ -622,19 +643,18 @@
         + [dma((2 * deep,))] * 2
         + [dma] * 2,
         compiler_params=pltpu.CompilerParams(
-            collective_id=1, has_side_effects=True, vmem_limit_bytes=30 * 2**20
+            collective_id=1, has_side_effects=True, vmem_limit_bytes=40 * 2**20
         ),
     )(*arguments)
-    whole = shape(width * rows, levels)
-    buffer = pltpu.VMEM((width * rows, levels), F32)
+    size = min(256, width * rows)
     outs = pl.pallas_call(
-        final_kernel,
+        functools.partial(final_kernel, size),
         out_shape=[whole] * 3,
         in_specs=[VM] * 8,
         out_specs=[ANY] * 3,
-        scratch_shapes=[buffer] * 3 + [dma((3, width // min(32, width)))],
-        compiler_params=pltpu.CompilerParams(vmem_limit_bytes=20 * 2**20),
-    )(tot, r_ext, v0, v1, v2, w0, w1, w2)
+        scratch_shapes=[pltpu.VMEM((width * rows, levels), F32)] * 2 + [dma, dma((2, width * rows // size))],
+        compiler_params=pltpu.CompilerParams(vmem_limit_bytes=16 * 2**20),
+    )(tot, *flat)
     return tuple(x.reshape(width, rows, levels) for x in outs)
 
 

time: 44 us -> 42.6 us (0.968)
  Pallas kernels: 43.2 us -> 41.8 us
    pallas_call x2, Pallas kernels: 43.2 us -> 41.8 us  [the longest x1 39.9 us: body(): pl.pallas_call(functools.partial(step_kernel, lons, lats), out_shape=[who...]
where the time goes in v2:
time: 42.6 us; the launch traced here: 42.5 us
  Pallas kernels  41.8 us (98%)
  between operations  0.64 us (2%)
    pallas_call x1, Pallas kernels, body(): pl.pallas_call(functools.partial(step_kernel, lons, lats), out_shape=[who...  39.9 us
    pallas_call x1, Pallas kernels, body(): pl.pallas_call(functools.partial(final_kernel, size), out_shape=[whole] *...  1.95 us

profile of v2, /device:TPU:0, one launch (start us, length us, event | category | flops | bytes accessed | tf_op | source)
XLA Modules:
  0.0 42.5 jit_solution(6079465445641357834)
XLA Ops:
  0.6 39.9 %shard_map.103 = (f32[2048,128]{1,0:T(8,128)S(1)}, f32[2048,128]{1,0:T(8,128)S(1)}, f32[2048,128]{1,0:T(8,128)S(1)}, f32[2048,128]{1,0:T(8,128)S(1)}, f32[2048,1...) custom-call(s32[8]{0:T(128)} %refs_0_.1, f32[8]{0:T(128)} %refs_1_.1, ...), custom_call_target="tpu_custom_call" | custom-call | tf_op jit(solution)/shard_map/pallas_call | solution.py:605
  40.5 2.0 %shard_map.104 = (f32[2048,128]{1,0:T(8,128)}, f32[2048,128]{1,0:T(8,128)}, f32[2048,128]{1,0:T(8,128)}) custom-call(f32[8,128]{1,0:T(8,128)S(1)} %get-tuple-element.14.tot, f32[2048,128]{1,0:T(8,128)S(1)} %get-tuple-element.15.r, f32[2048,128]{1,0:T(8,128)S(1)} %get-tuple-element.16.v0, f32[2048,128]{1,0:T(8,128)S(1)} %get-tuple-element.17.v1, ...), custom_call_target="tpu_custom_call" | custom-call | tf_op jit(solution)/shard_map/pallas_call | solution.py:650

commit v3 on v2

--- a/solution.py
+++ b/solution.py
@@ -109,7 +109,7 @@
     (t, double, s_buf, v_buf, g_buf, f_buf, inv_ext, met), refs = refs[:8], refs[8:]
     (column, packed, extra, lhs, part, every), refs = refs[:6], refs[6:]
     (off, f_lon, f_lat, f_lev, metric, vc_ref, c_sem), refs = refs[:7], refs[7:]
-    (t_sem, i_sem, hs, hr, ns, nr, p1s, p1r, p2s, p2r, ws, wr, es, er, fs, fr, rs, rr) = refs
+    (t_sem, i_sem, hs, hr, ns, nr, p1s, p1r, p2s, p2r, fs, fr, rs, rr) = refs
     width, rows, levels = tracer.shape
     quarter = width // lons
     deep = DEEP
@@ -127,7 +127,7 @@
         index = lax.rem(mine + k, devices)
         return {"lon": lax.div(index, lats), "lat": lax.rem(index, lats)}
 
-    first_rows = [rows - 1, 0, 1] + list(range(2, rows - 1))
+    first_rows = [0, 1, 2, 3, rows - 1] + list(range(4, rows - 1))
     loads = {j: pltpu.make_async_copy(tracer.at[:, j, :], t.at[j + 1], t_sem.at[j]) for j in range(rows)}
     for j in first_rows:
         loads[j].start()
@@ -141,12 +141,19 @@
     matrices.start()
 
     barrier = pltpu.get_barrier_semaphore()
-    lax.fori_loop(1, devices, lambda k, c: (signal(barrier, peer_of(k)), c)[1], 0)
-
-    for copy in fetches:
-        copy.wait()
-    for j in range(rows):
-        met[deep + j : deep + j + 1, :] = jnp.full((1, levels), metric[j], F32)
+    def others():
+        far = lambda n: sorted(range(n), key=lambda k: abs(k - n // 2))
+        for b in far(lats):
+            for a in far(lons):
+                if a or b:
+                    yield {"lon": ring(a), "lat": lax.rem(lat + b, lats)}
+
+    unrolled = devices <= 64
+    if unrolled:
+        for peer in others():
+            signal(barrier, peer)
+    else:
+        lax.fori_loop(1, devices, lambda k, c: (signal(barrier, peer_of(k)), c)[1], 0)
 
     def clear_pads():
         for j in range(rows):
@@ -160,19 +167,18 @@
     def clear(ref, first, count):
         ref[first : first + count] = jnp.zeros((count,) + ref.shape[1:], F32)
 
-    @pl.when(jnp.logical_not(has_low))
-    def _():
-        clear(t, 0, 1)
-        clear(r_ext, 0, deep)
-        clear(inv_ext, 0, deep)
-        met[:deep, :] = jnp.zeros((deep, levels), F32)
-
-    @pl.when(jnp.logical_not(has_high))
-    def _():
-        clear(t, rows + 1, 2)
-        clear(r_ext, deep + rows, deep)
-        clear(inv_ext, deep + rows, deep)
-        met[deep + rows : ext, :] = jnp.zeros((deep, levels), F32)
+    def clear_sides():
+        @pl.when(jnp.logical_not(has_low))
+        def _():
+            clear(r_ext, 0, deep)
+            clear(inv_ext, 0, deep)
+            met[:deep, :] = jnp.zeros((deep, levels), F32)
+
+        @pl.when(jnp.logical_not(has_high))
+        def _():
+            clear(r_ext, deep + rows, deep)
+            clear(inv_ext, deep + rows, deep)
+            met[deep + rows : ext, :] = jnp.zeros((deep, levels), F32)
 
     up_row = remote(t.at[rows], t.at[0], hs.at[0], hr.at[0], above)
     down_rows = remote(t.at[pl.ds(1, 2)], t.at[pl.ds(rows + 1, 2)], hs.at[1], hr.at[1], below)
@@ -185,21 +191,6 @@
         remote(met.at[deep + m], met.at[deep + rows + m], ns.at[deep + m], nr.at[deep + m], below)
         for m in range(deep)
     ]
-    for j in first_rows[:3]:
-        loads[j].wait()
-    pl.semaphore_wait(barrier, devices - 1)
-
-    @pl.when(has_high)
-    def _():
-        up_row.start()
-
-    @pl.when(has_low)
-    def _():
-        down_rows.start()
-
-    for j in first_rows[3:]:
-        loads[j].wait()
-
     def mix(j):
         a = cubic_weights(f_lat[j])
         b = cubic_weights(f_lev[j])
@@ -248,47 +239,44 @@
                 x = [jnp.where(mask, x[(d - bit) % lons], x[d]) for d in range(lons)]
                 bit //= 2
             for d in range(lons):
-                g_buf[j, d, pl.ds(first, size), :] = x[d]
-        here = pl.ds(pl.multiple_of(2 * PAD + begin, PAD), quarter)
-        west = pl.ds(PAD, PAD)
-        east = pl.ds(2 * PAD + width, PAD)
-        for k in range(1, lons):
-            d = ring(k)
-            remote(g_buf.at[j, d], f_buf.at[j, here], p2s.at[j], p2r.at[j], {"lon": d}).start()
-        f_buf[j, here, :] = g_buf[j, me]
-        part = lax.rem(me + j, lons)
-
-        @pl.when(part == lons - 1)
-        def _():
+                g_buf[j, d, pl.ds(PAD + first, size), :] = x[d]
+        for d in range(lons):
+            g_buf[j, d, :PAD, :] = g_buf[j, (d + 1) % lons, PAD : 2 * PAD, :]
+            g_buf[j, d, PAD + quarter :, :] = g_buf[j, (d - 1) % lons, quarter : PAD + quarter, :]
+        slot = lax.rem(me + j, lons)
+
+        def give(skip, size):
+            there = pl.ds(pl.multiple_of(PAD + begin + skip, PAD), size)
             for k in range(1, lons):
-                src = g_buf.at[j, ring(k - 1), pl.ds(quarter - PAD, PAD)]
-                remote(src, f_buf.at[j, west], ws.at[j], wr.at[j], {"lon": ring(k)}).start()
-            f_buf[j, west, :] = g_buf[j, ring(-1), quarter - PAD :, :]
-
-        @pl.when(part == 0)
-        def _():
-            for k in range(1, lons):
-                src = g_buf.at[j, ring(k + 1), pl.ds(0, PAD)]
-                remote(src, f_buf.at[j, east], es.at[j], er.at[j], {"lon": ring(k)}).start()
-            f_buf[j, east, :] = g_buf[j, ring(1), :PAD, :]
-
-    def edge_wait(j, send_sem, recv_sem, owner, count):
-        block = f_buf.at[j, pl.ds(PAD, PAD * count)]
-        return remote(block, block, send_sem, recv_sem, {"lon": ring(1)})
+                d = ring(k)
+                src = g_buf.at[j, d, pl.ds(skip, size)]
+                remote(src, f_buf.at[j, there], p2s.at[j], p2r.at[j], {"lon": d}).start()
+            f_buf[j, there, :] = g_buf[j, me, skip : skip + size, :]
+
+        by_slot(slot, lambda: give(0, PAD + quarter), lambda: give(PAD, PAD + quarter), lambda: give(PAD, quarter))
+
+    def by_slot(slot, low_end, high_end, between):
+        pl.when(slot == 0)(low_end)
+        pl.when(slot == lons - 1)(high_end)
+        pl.when((slot > 0) & (slot < lons - 1))(between)
+
+    def count_of(j, size):
+        block = f_buf.at[j, pl.ds(0, size)]
+        return remote(block, block, p2s.at[j], p2r.at[j], {"lon": ring(1)})
 
     def arrive(j):
-        main = f_buf.at[j, pl.ds(2 * PAD, (lons - 1) * quarter)]
-        remote(main, main, p2s.at[j], p2r.at[j], {"lon": ring(1)}).wait_recv()
-        part = lax.rem(me + j, lons)
-
-        @pl.when(part != lons - 1)
-        def _():
-            edge_wait(j, ws.at[j], wr.at[j], lons - 1, 1).wait_recv()
-
-        @pl.when(part != 0)
-        def _():
-            edge_wait(j, es.at[j], er.at[j], 0, 1).wait_recv()
-
+        slot = lax.rem(me + j, lons)
+        most = (lons - 1) * quarter
+        by_slot(
+            slot,
+            lambda: count_of(j, most + PAD).wait_recv(),
+            lambda: count_of(j, most + PAD).wait_recv(),
+            lambda: count_of(j, most + 2 * PAD).wait_recv(),
+        )
+        east = f_buf[j, PAD : 2 * PAD, :]
+        west = f_buf[j, 2 * PAD + width : 3 * PAD + width, :]
+        f_buf[j, PAD : 2 * PAD, :] = west
+        f_buf[j, 2 * PAD + width : 3 * PAD + width, :] = east
         c = cubic_weights(f_lon[j])
         for first, size in pieces(0, wide, 64):
             r_ext[deep + j, pl.ds(first, size), :] = sum(
@@ -311,17 +299,14 @@
         return remote(r_ext.at[deep + j], r_ext.at[m], fs.at[deep + m], fr.at[deep + m], above)
 
     def settle(j):
-        all_of(g_buf, j, lons - 1, p2s.at[j], p2r.at[j]).wait_send()
         all_of(v_buf, j, lons - 1, p1s.at[j], p1r.at[j]).wait_send()
-        part = lax.rem(me + j, lons)
-
-        @pl.when(part == lons - 1)
-        def _():
-            edge_wait(j, ws.at[j], wr.at[j], lons - 1, lons - 1).wait_send()
-
-        @pl.when(part == 0)
-        def _():
-            edge_wait(j, es.at[j], er.at[j], 0, lons - 1).wait_send()
+        slot = lax.rem(me + j, lons)
+
+        def sent(size):
+            block = g_buf.at[j, pl.ds(0, lons - 1), pl.ds(0, size)]
+            return lambda: remote(block, block, p2s.at[j], p2r.at[j], {"lon": ring(1)}).wait_send()
+
+        by_slot(slot, sent(PAD + quarter), sent(PAD + quarter), sent(quarter))
 
     ws_refs, vs_refs, zs_refs = (w0, w1, w2), (v0, v1, v2), (z0, z1, z2)
     acc = [jnp.zeros((8, levels), F32) for _ in range(9)]
@@ -336,7 +321,8 @@
 
     def pack(e):
         matrix = inv_ext[e]
-        applied = column[0] * matrix - column[1] * pltpu.roll(matrix, levels - 1, 0)
+        middle = column[0] + 2.0 * met[e : e + 1, :]
+        applied = middle * matrix - column[1] * pltpu.roll(matrix, levels - 1, 0)
         applied = applied - column[2] * pltpu.roll(matrix, 1, 0)
         for n, x in enumerate((matrix, applied)):
             high, low = split(x)
@@ -368,11 +354,9 @@
         n = e - k
         m = met[e : e + 1, :]
         at = pl.ds(first + PAD, size)
-        result = zs_refs[k][n - 1, pl.ds(first, size), :] + (2.0 * m) * w[n, at, :]
-        result = result - m * (
-            w[n, pl.ds(first + PAD + 1, size), :] + w[n, pl.ds(first + PAD - 1, size), :]
-        )
-        return result - (w[n - 1, at, :] + w[n + 1, at, :])
+        sides = w[n, pl.ds(first + PAD + 1, size), :] + w[n, pl.ds(first + PAD - 1, size), :]
+        result = zs_refs[k][n - 1, pl.ds(first, size), :] - (w[n - 1, at, :] + w[n + 1, at, :])
+        return result - m * sides
 
     pairs = {0: ((0, "r", 0), (3, 0, 0)), 1: ((1, "r", 1), (4, 0, 1), (6, 1, 1)),
              2: ((2, "r", 2), (5, 0, 2), (7, 1, 2), (8, 2, 2))}
@@ -411,9 +395,18 @@
     order += [j for j in range(rows) if j not in order]
     outer = sorted(edges, key=lambda j: min(j, rows - 1 - j))
     later = outer + [j for j in range(rows) if j not in outer]
+    for copy in fetches:
+        copy.wait()
+    here = set()
+
+    def need(*wanted):
+        for j in first_rows:
+            if j in wanted and j not in here:
+                here.add(j)
+                loads[j].wait()
+
     waited = False
-    sent_inv = False
-    for j in order:
+    for n, j in enumerate(order):
         if not plain(j) and not waited:
             waited = True
 
@@ -425,10 +418,33 @@
             def _():
                 down_rows.wait_recv()
 
+        need(*range(j - 1, j + 3))
         mix(j)
+        if n == 0:
+            pl.semaphore_wait(barrier, devices - 1)
         spread(j)
-        if not sent_inv:
-            sent_inv = True
+        if n == 0:
+            need(0, 1, rows - 1)
+
+            @pl.when(has_high)
+            def _():
+                up_row.start()
+
+            @pl.when(has_low)
+            def _():
+                down_rows.start()
+
+            @pl.when(jnp.logical_not(has_low))
+            def _():
+                clear(t, 0, 1)
+
+            @pl.when(jnp.logical_not(has_high))
+            def _():
+                clear(t, rows + 1, 2)
+
+        if n == 1:
+            for m in range(rows):
+                met[deep + m : deep + m + 1, :] = jnp.full((1, levels), metric[m], F32)
             matrices.wait()
 
             @pl.when(has_high)
@@ -443,6 +459,7 @@
                 for copy in down_met:
                     copy.start()
 
+    clear_sides()
     clear_pads()
     turn_coefficients()
     for j in later:
@@ -520,22 +537,14 @@
     part[...] = row
     every[mine] = row
 
-    def tell(a, b):
-        to = {"lon": ring(a), "lat": lax.rem(lat + b, lats)}
-        remote(part, every.at[mine], rs, rr, to).start()
-
-    def tell_rest(k, carry):
-        remote(part, every.at[mine], rs, rr, peer_of(k)).start()
-        return carry
-
-    if devices <= 64:
-        far = lambda n, count: sorted(range(n), key=lambda k: abs(k - n // 2))
-        for b in far(lats, lats):
-            for a in far(lons, lons):
-                if a or b:
-                    tell(a, b)
+    def tell(peer):
+        remote(part, every.at[mine], rs, rr, peer).start()
+
+    if unrolled:
+        for peer in others():
+            tell(peer)
     else:
-        lax.fori_loop(1, devices, tell_rest, 0)
+        lax.fori_loop(1, devices, lambda k, c: (tell(peer_of(k)), c)[1], 0)
     for j in range(rows):
         where = pl.ds(j, width, stride=rows)
         flat[0][where, :] = r_ext[deep + j, pl.ds(PAD, width), :]
@@ -563,8 +572,8 @@
         for m in range(deep):
             low_copy(m).wait_send()
 
-    others = every.at[pl.ds(0, devices - 1)]
-    totals = remote(others, others, rs, rr, {"lon": ring(1)})
+    most = every.at[pl.ds(0, devices - 1)]
+    totals = remote(most, most, rs, rr, {"lon": ring(1)})
     totals.wait_recv()
     totals.wait_send()
     tot[...] = jnp.broadcast_to(jnp.sum(every[...], axis=0), tot.shape)
@@ -616,7 +625,7 @@
             pltpu.VMEM((2, 2 * width, levels), F32),
             pltpu.VMEM((rows, width, levels), F32),
             pltpu.VMEM((rows, lons, quarter, levels), F32),
-            pltpu.VMEM((rows, lons, quarter, levels), F32),
+            pltpu.VMEM((rows, lons, quarter + 2 * PAD, levels), F32),
             pltpu.VMEM((rows, wide + 2 * PAD, levels), F32),
             pltpu.VMEM((ext, levels, levels), F32),
             pltpu.VMEM((ext, levels), F32),
@@ -639,14 +648,14 @@
             dma((2 * deep,)),
             dma((2 * deep,)),
         ]
-        + [dma((rows,))] * 8
+        + [dma((rows,))] * 4
         + [dma((2 * deep,))] * 2
         + [dma] * 2,
         compiler_params=pltpu.CompilerParams(
             collective_id=1, has_side_effects=True, vmem_limit_bytes=40 * 2**20
         ),
     )(*arguments)
-    size = min(256, width * rows)
+    size = min(512, width * rows)
     outs = pl.pallas_call(
         functools.partial(final_kernel, size),
         out_shape=[whole] * 3,

time: 42.6 us -> 42.1 us (0.988)
  Pallas kernels: 41.8 us -> 41.3 us
where the time goes in v3:
time: 42.1 us; the launch traced here: 42 us
  Pallas kernels  41.3 us (98%)
  between operations  0.64 us (2%)
    pallas_call x1, Pallas kernels, body(): pl.pallas_call(functools.partial(step_kernel, lons, lats), out_shape=[who...  39.6 us
    pallas_call x1, Pallas kernels, body(): pl.pallas_call(functools.partial(final_kernel, size), out_shape=[whole] *...  1.74 us

profile of v3, /device:TPU:0, one launch (start us, length us, event | category | flops | bytes accessed | tf_op | source)
XLA Modules:
  0.0 42.0 jit_solution(11355984083566185230)
XLA Ops:
  0.6 39.6 %shard_map.103 = (f32[2048,128]{1,0:T(8,128)S(1)}, f32[2048,128]{1,0:T(8,128)S(1)}, f32[2048,128]{1,0:T(8,128)S(1)}, f32[2048,128]{1,0:T(8,128)S(1)}, f32[2048,1...) custom-call(s32[8]{0:T(128)} %refs_0_.1, f32[8]{0:T(128)} %refs_1_.1, ...), custom_call_target="tpu_custom_call" | custom-call | tf_op jit(solution)/shard_map/pallas_call | solution.py:614
  40.2 1.7 %shard_map.104 = (f32[2048,128]{1,0:T(8,128)}, f32[2048,128]{1,0:T(8,128)}, f32[2048,128]{1,0:T(8,128)}) custom-call(f32[8,128]{1,0:T(8,128)S(1)} %get-tuple-element.14.tot, f32[2048,128]{1,0:T(8,128)S(1)} %get-tuple-element.15.r, f32[2048,128]{1,0:T(8,128)S(1)} %get-tuple-element.16.v0, f32[2048,128]{1,0:T(8,128)S(1)} %get-tuple-element.17.v1, ...), custom_call_target="tpu_custom_call" | custom-call | tf_op jit(solution)/shard_map/pallas_call | solution.py:659

commit v4 on v3

--- a/solution.py
+++ b/solution.py
@@ -109,7 +109,7 @@
     (t, double, s_buf, v_buf, g_buf, f_buf, inv_ext, met), refs = refs[:8], refs[8:]
     (column, packed, extra, lhs, part, every), refs = refs[:6], refs[6:]
     (off, f_lon, f_lat, f_lev, metric, vc_ref, c_sem), refs = refs[:7], refs[7:]
-    (t_sem, i_sem, hs, hr, ns, nr, p1s, p1r, p2s, p2r, fs, fr, rs, rr) = refs
+    (t_sem, i_sem, hs, hr, ns, nr, p1s, p1r, p2s, p2r, fs, fr, rs, rr, word) = refs
     width, rows, levels = tracer.shape
     quarter = width // lons
     deep = DEEP
@@ -149,11 +149,40 @@
                     yield {"lon": ring(a), "lat": lax.rem(lat + b, lats)}
 
     unrolled = devices <= 64
-    if unrolled:
-        for peer in others():
-            signal(barrier, peer)
-    else:
-        lax.fori_loop(1, devices, lambda k, c: (signal(barrier, peer_of(k)), c)[1], 0)
+    for k in range(1, lons):
+        signal(barrier, {"lon": ring(k)})
+
+    @pl.when(has_low)
+    def _():
+        signal(barrier, below)
+
+    @pl.when(has_high)
+    def _():
+        signal(barrier, above)
+
+    def pass_along_lat():
+        @pl.when(jnp.logical_not(has_high))
+        def _():
+            signal(word.at[1], below)
+
+        @pl.when(has_low)
+        def _():
+            pl.semaphore_wait(word.at[0], 1)
+
+        @pl.when(has_high)
+        def _():
+            signal(word.at[0], above)
+            pl.semaphore_wait(word.at[1], 1)
+
+        @pl.when(has_low & has_high)
+        def _():
+            signal(word.at[1], below)
+
+    def pass_over_lon():
+        for k in range(1, lons):
+            signal(word.at[2], {"lon": ring(k)})
+        pl.semaphore_wait(word.at[2], lons - 1)
+
 
     def clear_pads():
         for j in range(rows):
@@ -421,7 +450,7 @@
         need(*range(j - 1, j + 3))
         mix(j)
         if n == 0:
-            pl.semaphore_wait(barrier, devices - 1)
+            pl.semaphore_wait(barrier, (lons - 1) + has_low.astype(jnp.int32) + has_high.astype(jnp.int32))
         spread(j)
         if n == 0:
             need(0, 1, rows - 1)
@@ -462,8 +491,10 @@
     clear_sides()
     clear_pads()
     turn_coefficients()
+    pass_along_lat()
     for j in later:
         deliver(j)
+    pass_over_lon()
     for e in range(deep, deep + rows):
         pack(e)
 
@@ -650,7 +681,8 @@
         ]
         + [dma((rows,))] * 4
         + [dma((2 * deep,))] * 2
-        + [dma] * 2,
+        + [dma] * 2
+        + [pltpu.SemaphoreType.REGULAR((3,))],
         compiler_params=pltpu.CompilerParams(
             collective_id=1, has_side_effects=True, vmem_limit_bytes=40 * 2**20
         ),

time: 42.1 us -> 40.8 us (0.969)
  Pallas kernels: 41.3 us -> 40 us
    pallas_call x1, Pallas kernels: 39.6 us -> 38.2 us  [body(): pl.pallas_call(functools.partial(step_kernel, lons, lats), out_shape=[who...]
where the time goes in v4:
time: 40.8 us; the launch traced here: 40.6 us
  Pallas kernels  40 us (98%)
  between operations  0.64 us (2%)
    pallas_call x1, Pallas kernels, body(): pl.pallas_call(functools.partial(step_kernel, lons, lats), out_shape=[who...  38.2 us
    pallas_call x1, Pallas kernels, body(): pl.pallas_call(functools.partial(final_kernel, size), out_shape=[whole] *...  1.74 us

profile of v4, /device:TPU:0, one launch (start us, length us, event | category | flops | bytes accessed | tf_op | source)
XLA Modules:
  0.0 40.6 jit_solution(4780208896043757342)
XLA Ops:
  0.6 38.2 %shard_map.103 = (f32[2048,128]{1,0:T(8,128)S(1)}, f32[2048,128]{1,0:T(8,128)S(1)}, f32[2048,128]{1,0:T(8,128)S(1)}, f32[2048,128]{1,0:T(8,128)S(1)}, f32[2048,1...) custom-call(s32[8]{0:T(128)} %refs_0_.1, f32[8]{0:T(128)} %refs_1_.1, ...), custom_call_target="tpu_custom_call" | custom-call | tf_op jit(solution)/shard_map/pallas_call | solution.py:645
  38.9 1.7 %shard_map.104 = (f32[2048,128]{1,0:T(8,128)}, f32[2048,128]{1,0:T(8,128)}, f32[2048,128]{1,0:T(8,128)}) custom-call(f32[8,128]{1,0:T(8,128)S(1)} %get-tuple-element.14.tot, f32[2048,128]{1,0:T(8,128)S(1)} %get-tuple-element.15.r, f32[2048,128]{1,0:T(8,128)S(1)} %get-tuple-element.16.v0, f32[2048,128]{1,0:T(8,128)S(1)} %get-tuple-element.17.v1, ...), custom_call_target="tpu_custom_call" | custom-call | tf_op jit(solution)/shard_map/pallas_call | solution.py:691

commit v5 on v4

--- a/solution.py
+++ b/solution.py
@@ -107,7 +107,7 @@
     flat, tot, refs = refs[:7], refs[7], refs[8:]
     (r_ext, v0, v1, v2, w0, w1, w2, z0, z1, z2), refs = refs[:10], refs[10:]
     (t, double, s_buf, v_buf, g_buf, f_buf, inv_ext, met), refs = refs[:8], refs[8:]
-    (column, packed, extra, lhs, part, every), refs = refs[:6], refs[6:]
+    (column, packed, extra, packed_far, extra_far, lhs, part, every), refs = refs[:8], refs[8:]
     (off, f_lon, f_lat, f_lev, metric, vc_ref, c_sem), refs = refs[:7], refs[7:]
     (t_sem, i_sem, hs, hr, ns, nr, p1s, p1r, p2s, p2r, fs, fr, rs, rr, word) = refs
     width, rows, levels = tracer.shape
@@ -141,13 +141,6 @@
     matrices.start()
 
     barrier = pltpu.get_barrier_semaphore()
-    def others():
-        far = lambda n: sorted(range(n), key=lambda k: abs(k - n // 2))
-        for b in far(lats):
-            for a in far(lons):
-                if a or b:
-                    yield {"lon": ring(a), "lat": lax.rem(lat + b, lats)}
-
     unrolled = devices <= 64
     for k in range(1, lons):
         signal(barrier, {"lon": ring(k)})
@@ -360,6 +353,30 @@
             packed[e, at, levels:] = high
             extra[e, at, :] = low
 
+    def pack_far(side, near):
+        product = inv_ext[near[0]]
+        for e in near[1:]:
+            product = jnp.dot(product, inv_ext[e], precision=lax.Precision.HIGHEST, preferred_element_type=F32)
+        high, low = split(product)
+        packed_far[side, :, :levels] = high
+        packed_far[side, :, levels:] = high
+        extra_far[side] = low
+
+    def far_row(side, e, inner, slot):
+        dims = (((1,), (1,)), ((), ()))
+        for first, size in pieces(0, wide, lines):
+            load_lhs(slot, first, size, r_ext[e, pl.ds(first, size), :])
+        change = lax.dot_general(lhs[slot], packed_far[side], dims, preferred_element_type=F32)
+        change = change + lax.dot_general(
+            lhs[slot, :, :levels], extra_far[side], dims, preferred_element_type=F32
+        )
+        sign = 1.0 if deep % 2 else -1.0
+        for first, size in pieces(PAD, PAD + width, lines):
+            at = pl.ds(first, size)
+            v = v2[inner - deep, at, :] - sign * change[first : first + size]
+            v2[inner - deep, at, :] = v
+            gather(ITERS - 1, inner, first, size, v)
+
     def solve(k, e, slot):
         dims = (((1,), (1,)), ((), ()))
         both = lax.dot_general(lhs[slot], packed[e], dims, preferred_element_type=F32)
@@ -406,7 +423,8 @@
             for first, size in pieces(PAD, PAD + width, lines):
                 v = stencil(k, e, first, size)
                 vs_refs[k][e - deep, pl.ds(first, size), :] = v
-                gather(k, e, first, size, v)
+                if deep < e < deep + rows - 1:
+                    gather(k, e, first, size, v)
 
     def gather(k, e, first, size, v):
         for n, p, q in pairs[k]:
@@ -420,8 +438,9 @@
 
     plain = lambda j: 1 <= j <= rows - 3
     edges = [j for j in range(rows) if j < deep or j >= rows - deep]
-    order = [j for j in edges if plain(j)] + [j for j in edges if not plain(j)]
-    order += [j for j in range(rows) if j not in order]
+    inner = [j for j in range(rows) if j not in edges]
+    reach = [j for j in edges if j == 0] + [j for j in reversed(edges) if j > rows - 3]
+    order = [j for j in edges if plain(j)] + reach[:1] + inner[:1] + reach[1:] + inner[1:]
     outer = sorted(edges, key=lambda j: min(j, rows - 1 - j))
     later = outer + [j for j in range(rows) if j not in outer]
     for copy in fetches:
@@ -434,19 +453,14 @@
                 here.add(j)
                 loads[j].wait()
 
-    waited = False
+    low_here = high_here = False
     for n, j in enumerate(order):
-        if not plain(j) and not waited:
-            waited = True
-
-            @pl.when(has_low)
-            def _():
-                up_row.wait_recv()
-
-            @pl.when(has_high)
-            def _():
-                down_rows.wait_recv()
-
+        if j == 0 and not low_here:
+            low_here = True
+            pl.when(has_low)(lambda: up_row.wait_recv())
+        if j > rows - 3 and not high_here:
+            high_here = True
+            pl.when(has_high)(lambda: down_rows.wait_recv())
         need(*range(j - 1, j + 3))
         mix(j)
         if n == 0:
@@ -510,8 +524,12 @@
         for copy in down_met:
             copy.wait_recv()
 
-    for e in list(range(deep)) + list(range(deep + rows, ext)):
+    for e in list(range(1, deep)) + list(range(deep + rows, ext - 1)):
         pack(e)
+    pack_far(0, range(deep - 1, -1, -1))
+    pack_far(1, range(deep + rows, ext))
+    clear(w0, 0, 1)
+    clear(w0, ext - 1, 1)
 
     done = {}
     slots = [0]
@@ -546,9 +564,13 @@
         def _():
             low_copy(m).wait_recv()
 
-        for e in (deep - 1 - m, deep + rows + m):
-            first_solve(e)
-
+        for side, e in enumerate((deep - 1 - m, deep + rows + m)):
+            if m < deep - 1:
+                first_solve(e)
+            else:
+                far_row(side, e, (deep, deep + rows - 1)[side], slot())
+
+    done["w", 0, 0] = done["w", 0, ext - 1] = True
     for n, j in enumerate(outer):
         arrive(j)
         first_solve(deep + j)
@@ -560,7 +582,6 @@
         first_solve(deep + j)
         ready()
     halo_rows(deep - 1)
-    ready()
 
     row = jnp.zeros((1, levels), F32)
     for n in range(9):
@@ -572,8 +593,14 @@
         remote(part, every.at[mine], rs, rr, peer).start()
 
     if unrolled:
-        for peer in others():
-            tell(peer)
+        for n in range(lats):
+            row_of = jnp.where(lat >= lats // 2, n, lats - 1 - n)
+            for a in range(1, lons):
+                tell({"lon": ring(a), "lat": row_of})
+
+            @pl.when(row_of != lat)
+            def _():
+                tell({"lat": row_of})
     else:
         lax.fori_loop(1, devices, lambda k, c: (tell(peer_of(k)), c)[1], 0)
     for j in range(rows):
@@ -663,6 +690,8 @@
             pltpu.VMEM((3, levels, levels), F32),
             pltpu.VMEM((ext, 2 * levels, 2 * levels), BF16),
             pltpu.VMEM((ext, 2 * levels, levels), BF16),
+            pltpu.VMEM((2, levels, 2 * levels), BF16),
+            pltpu.VMEM((2, levels, levels), BF16),
             pltpu.VMEM((2, wide, 2 * levels), BF16),
             pltpu.VMEM((1, levels), F32),
             pltpu.VMEM((devices, 1, levels), F32),

time: 40.8 us -> 40.6 us (level)
  no operation moved by 1% of the time
where the time goes in v5:
time: 40.6 us; the launch traced here: 40.5 us
  Pallas kernels  39.8 us (98%)
  between operations  0.64 us (2%)
    pallas_call x1, Pallas kernels, body(): pl.pallas_call(functools.partial(step_kernel, lons, lats), out_shape=[who...  38.1 us
    pallas_call x1, Pallas kernels, body(): pl.pallas_call(functools.partial(final_kernel, size), out_shape=[whole] *...  1.74 us

profile of v5, /device:TPU:0, one launch (start us, length us, event | category | flops | bytes accessed | tf_op | source)
XLA Modules:
  0.0 40.5 jit_solution(13507744553235812761)
XLA Ops:
  0.6 38.1 %shard_map.103 = (f32[2048,128]{1,0:T(8,128)S(1)}, f32[2048,128]{1,0:T(8,128)S(1)}, f32[2048,128]{1,0:T(8,128)S(1)}, f32[2048,128]{1,0:T(8,128)S(1)}, f32[2048,1...) custom-call(s32[8]{0:T(128)} %refs_0_.1, f32[8]{0:T(128)} %refs_1_.1, ...), custom_call_target="tpu_custom_call" | custom-call | tf_op jit(solution)/shard_map/pallas_call | solution.py:672
  38.7 1.7 %shard_map.104 = (f32[2048,128]{1,0:T(8,128)}, f32[2048,128]{1,0:T(8,128)}, f32[2048,128]{1,0:T(8,128)}) custom-call(f32[8,128]{1,0:T(8,128)S(1)} %get-tuple-element.14.tot, f32[2048,128]{1,0:T(8,128)S(1)} %get-tuple-element.15.r, f32[2048,128]{1,0:T(8,128)S(1)} %get-tuple-element.16.v0, f32[2048,128]{1,0:T(8,128)S(1)} %get-tuple-element.17.v1, ...), custom_call_target="tpu_custom_call" | custom-call | tf_op jit(solution)/shard_map/pallas_call | solution.py:720

commit v6 on v5

--- a/solution.py
+++ b/solution.py
@@ -116,6 +116,7 @@
     ext, wide = rows + 2 * deep, width + 2 * PAD
     me, lat = lax.axis_index("lon"), lax.axis_index("lat")
     ring = lambda k: lax.rem(me + (k + lons), lons)
+    turns = sorted(range(1, lons), key=lambda k: (k + 1) % 2)
     has_low, has_high = lat > 0, lat < lats - 1
     below = {"lat": lax.max(lat - 1, 0)}
     above = {"lat": lax.min(lat + 1, lats - 1)}
@@ -237,7 +238,7 @@
         return remote(ref.at[j, pl.ds(0, count)], ref.at[j, pl.ds(0, count)], send_sem, recv_sem, {"lon": ring(1)})
 
     def spread(j):
-        for k in range(1, lons):
+        for k in turns:
             q = ring(k)
             remote(
                 s_buf.at[j, pl.ds(part_of(q, j), quarter)], v_buf.at[j, me], p1s.at[j], p1r.at[j], {"lon": q}
@@ -269,7 +270,7 @@
 
         def give(skip, size):
             there = pl.ds(pl.multiple_of(PAD + begin + skip, PAD), size)
-            for k in range(1, lons):
+            for k in turns:
                 d = ring(k)
                 src = g_buf.at[j, d, pl.ds(skip, size)]
                 remote(src, f_buf.at[j, there], p2s.at[j], p2r.at[j], {"lon": d}).start()

time: 40.6 us -> 40.6 us (level)
  no operation moved by 1% of the time
where the time goes in v6:
time: 40.6 us; the launch traced here: 40.5 us
  Pallas kernels  39.8 us (98%)
  between operations  0.64 us (2%)
    pallas_call x1, Pallas kernels, body(): pl.pallas_call(functools.partial(step_kernel, lons, lats), out_shape=[who...  38.1 us
    pallas_call x1, Pallas kernels, body(): pl.pallas_call(functools.partial(final_kernel, size), out_shape=[whole] *...  1.74 us

profile of v6, /device:TPU:0, one launch (start us, length us, event | category | flops | bytes accessed | tf_op | source)
XLA Modules:
  0.0 40.5 jit_solution(5782565232004854961)
XLA Ops:
  0.6 38.1 %shard_map.103 = (f32[2048,128]{1,0:T(8,128)S(1)}, f32[2048,128]{1,0:T(8,128)S(1)}, f32[2048,128]{1,0:T(8,128)S(1)}, f32[2048,128]{1,0:T(8,128)S(1)}, f32[2048,1...) custom-call(s32[8]{0:T(128)} %refs_0_.1, f32[8]{0:T(128)} %refs_1_.1, ...), custom_call_target="tpu_custom_call" | custom-call | tf_op jit(solution)/shard_map/pallas_call | solution.py:673
  38.7 1.7 %shard_map.104 = (f32[2048,128]{1,0:T(8,128)}, f32[2048,128]{1,0:T(8,128)}, f32[2048,128]{1,0:T(8,128)}) custom-call(f32[8,128]{1,0:T(8,128)S(1)} %get-tuple-element.14.tot, f32[2048,128]{1,0:T(8,128)S(1)} %get-tuple-element.15.r, f32[2048,128]{1,0:T(8,128)S(1)} %get-tuple-element.16.v0, f32[2048,128]{1,0:T(8,128)S(1)} %get-tuple-element.17.v1, ...), custom_call_target="tpu_custom_call" | custom-call | tf_op jit(solution)/shard_map/pallas_call | solution.py:721
